TPU v7x, 256 devices: a whole 4x4x8 slice. The times are simulated.
256 devices in a mesh: rep: 16 (over y, z_hi, core), tp: 16 (over x, z_lo).
Axes of the slice: x: 4, y: 4, z: 8 (z_hi: 2, z_lo: 4; z = z_hi * 4 + z_lo), core: 2. Of those that a mesh axis runs over, the one named last changes fastest.
Arguments:
- activations: bfloat16 [16, 2048, 4096], P('rep', 'tp'), may hold values from -6 to 6
- cotangent: bfloat16 [16, 2048, 8192], P('rep', None, 'tp'), may hold values from -0.13183594 to 0.13183594
- drift: bfloat16 [16, 4096, 8192], P('rep', None, 'tp'), may hold values from -8 to 8
- outer_weights: float32 [4096, 8192], P(('rep', 'tp')), may hold values from -6 to 6
- momentum: float32 [4096, 8192], P(('rep', 'tp')), may hold values from -6 to 6
Outputs:
- weights: bfloat16 [4096, 8192], P(None, 'tp')
- new_outer: float32 [4096, 8192], P(('rep', 'tp'))
- new_momentum: float32 [4096, 8192], P(('rep', 'tp'))
All inputs are finite; a program needn't handle non-finite values.
Results may differ from a plain program's by a relative error of at most 0.0085.
Values may be sent and summed in bfloat16 or wider, within the bound.
A program may use at most 128 MiB of HBM per device.

v0:
```python
import jax
import jax.numpy as jnp
from jax import lax
from jax.sharding import Mesh
from jax.sharding import PartitionSpec as P

TP = ("tp_0", "tp_1")
REP_TP = ("rep", "tp_0", "tp_1")
outer_rate = 0.7
nesterov = 0.9


def gathered_by_axis(shard, axes, dim):
    if not axes:
        return shard
    nearer = lax.all_gather(shard, axes[-1], axis=dim, tiled=True)
    return gathered_by_axis(nearer, axes[:-1], dim)


def on_device(activations, cotangent, drift, outer_weights, momentum):
    replicas = lax.axis_size("rep")
    cot_rows = cotangent[0]
    grad = jnp.einsum(
        "td,tf->df",
        gathered_by_axis(activations, TP, 1)[0],
        cot_rows,
        preferred_element_type=jnp.float32,
    )
    delta = lax.optimization_barrier((drift[0].astype(jnp.float32) + grad).astype(jnp.bfloat16))
    summed = lax.psum_scatter(
        delta.astype(jnp.float32).astype(jnp.bfloat16), "rep", scatter_dimension=0, tiled=True
    ).astype(jnp.float32)
    summed = lax.all_to_all(
        summed.astype(jnp.bfloat16), TP, split_axis=0, concat_axis=1, tiled=True
    ).astype(summed.dtype)
    average = summed / replicas
    new_momentum = nesterov * momentum + average
    new_outer = outer_weights - outer_rate * (average + nesterov * new_momentum)
    rounded = new_outer.astype(jnp.bfloat16)
    part = lax.all_to_all(rounded, TP, split_axis=1, concat_axis=0, tiled=True)
    weights = lax.all_gather(part, "rep", axis=0, tiled=True)
    return (weights, new_outer, new_momentum)


def solution(mesh):
    split = Mesh(mesh.devices.reshape(mesh.shape["rep"], 4, 4), ("rep", "tp_0", "tp_1"))
    in_specs = (
        P("rep", TP, None),
        P("rep", None, TP),
        P("rep", None, TP),
        P(REP_TP, None),
        P(REP_TP, None),
    )
    out_specs = (P(None, TP), P(REP_TP, None), P(REP_TP, None))
    return jax.shard_map(
        on_device, mesh=split, in_specs=in_specs, out_specs=out_specs, check_vma=False
    )
```

profile of v0, /device:TPU:1, one launch (start us, length us, event | category | flops | bytes accessed | tf_op | source)
XLA Modules:
  0.0 488.0 jit_solution(10202288569812770123)
XLA Ops:
  7.2 0.0 copy-start
  7.2 0.0 all-gather.4.cloned.1.call-start
  7.2 0.7 all-gather.4.cloned.1.call-update
  7.9 0.0 all-gather.6.cloned.1.call-start
  8.0 89.4 %all-gather.4.cloned.1.call-done = bf16[1,512,4096]{2,1,0:T(8,128)(2,1)} async-done(((bf16[1,128,4096]{2,1,0:T(8,128)(2,1)}), bf16[1,512,4096]{2,1,0:T(8,128)(2,1)}) %all-gather.4.cloned.1.call-update) | async-done | bytes 4194320 | tf_op jit(solution)/shard_map/all_gather | solution.py:16
  97.4 0.0 all-gather.6.cloned.1.call-update
  97.4 0.0 reduce-scatter.2.cloned.1.call-start
  97.4 158.5 %all-gather.6.cloned.1.call-done = bf16[1,2048,4096]{2,1,0:T(8,128)(2,1)} async-done(((bf16[1,512,4096]{2,1,0:T(8,128)(2,1)}), bf16[1,2048,4096]{2,1,0:T(8,128)(2,1)}) %all-gather.6.cloned.1.call-update) | async-done | bytes 16777232 | tf_op jit(solution)/shard_map/all_gather | solution.py:16
  255.9 0.0 copy-done
  255.9 14.4 %fusion.2 = bf16[4096,512]{1,0:T(8,128)(2,1)} fusion(bf16[1,2048,4096]{2,1,0:T(8,128)(2,1)} %all-gather.6.cloned.1.call-done, bf16[1,4096,512]{2,1,0:T(8,128)(2,1)} %param.7, bf16[1,2048,512]{2,1,0:T(8,128)(2,1)S(1)} %copy-done), kind=kOutput, calls=%fused_computation.3 | convolution fusion | flops 8596226048 | bytes 27262976 | tf_op jit(solution)/shard_map/td,tf->df/dot_general | solution.py:23
  270.4 0.0 copy-start.1
  270.4 0.0 copy-start.2
  270.4 0.0 reduce-scatter.2.cloned.1.call-update
  270.4 0.0 all-gather.8.cloned.1.call-start
  270.4 103.5 %reduce-scatter.2.cloned.1.call-done = bf16[256,512]{1,0:T(8,128)(2,1)} async-done(((bf16[4096,512]{1,0:T(8,128)(2,1)}), bf16[256,512]{1,0:T(8,128)(2,1)}) %reduce-scatter.2.cloned.1.call-update) | async-done | bytes 262160 | tf_op jit(solution)/shard_map/reduce_scatter | solution.py:30
  374.0 12.9 %all_to_all.32 = bf16[16,16,512]{2,1,0:T(8,128)(2,1)S(1)} all-to-all(bf16[16,16,512]{2,1,0:T(8,128)(2,1)} %bitcast.27), channel_id=1, replica_groups=mesh['rep'=16,'tp_0'=4,'tp_1'=4] {'tp_0','tp_1'}, dimensions={0} | all-to-all | bytes 524288 | tf_op jit(solution)/shard_map/all_to_all | solution.py:33
  386.9 0.1 multiply_bitcast_fusion
  387.0 0.0 copy-done.1
  387.0 0.0 copy-done.2
  387.0 1.1 fusion.6
  388.1 11.3 %all_to_all.33 = bf16[16,16,512]{2,0,1:T(8,128)(2,1)} all-to-all(bf16[16,16,512]{2,0,1:T(8,128)(2,1)S(1)} %bitcast.25), channel_id=1, replica_groups=mesh['rep'=16,'tp_0'=4,'tp_1'=4] {'tp_0','tp_1'}, dimensions={1} | all-to-all | bytes 524288 | tf_op jit(solution)/shard_map/all_to_all | solution.py:40
  399.4 0.0 all-gather.8.cloned.1.call-update
  399.5 77.6 %all-gather.8.cloned.1.call-done = bf16[4096,512]{1,0:T(8,128)(2,1)} async-done(((bf16[256,512]{1,0:T(8,128)(2,1)}), bf16[4096,512]{1,0:T(8,128)(2,1)}) %all-gather.8.cloned.1.call-update) | async-done | bytes 4194320 | tf_op jit(solution)/shard_map/all_gather | solution.py:41
  477.0 4.5 copy.18
  (2 shorter events, 0.1 us)
Async XLA Ops:
  7.2 248.8 %copy-start = (bf16[1,2048,512]{2,1,0:T(8,128)(2,1)S(1)}, bf16[1,2048,512]{2,1,0:T(8,128)(2,1)}, u32[]{:S(2)}) copy-start(bf16[1,2048,512]{2,1,0:T(8,128)(2,1)} %param.6) | copy-start | bytes 6291460
  7.2 90.2 %all-gather.4.cloned.1.call-start = ((), (), s32[]{:S(2)}) async-start(), calls=%async_computation.3 | async-start | bytes 5242880 | tf_op jit(solution)/shard_map/all_gather | solution.py:16
  7.9 248.0 %all-gather.6.cloned.1.call-start = ((), (), s32[]{:S(2)}) async-start(), calls=%async_computation.4 | async-start | bytes 20971520 | tf_op jit(solution)/shard_map/all_gather | solution.py:16
  97.4 276.6 %reduce-scatter.2.cloned.1.call-start = ((), (), s32[]{:S(2)}) async-start(), calls=%async_computation.5 | async-start | bytes 4456448 | tf_op jit(solution)/shard_map/reduce_scatter | solution.py:30
  270.4 116.6 %copy-start.1 = (f32[16,8192]{1,0:T(8,128)S(1)}, f32[16,8192]{1,0:T(8,128)}, u32[]{:S(2)}) copy-start(f32[16,8192]{1,0:T(8,128)} %param.8) | copy-start | bytes 1572868
  270.4 116.6 %copy-start.2 = (f32[16,8192]{1,0:T(8,128)S(1)}, f32[16,8192]{1,0:T(8,128)}, u32[]{:S(2)}) copy-start(f32[16,8192]{1,0:T(8,128)} %param.9) | copy-start | bytes 1572868
  270.4 206.6 %all-gather.8.cloned.1.call-start = ((), (), s32[]{:S(2)}) async-start(), calls=%async_computation.6 | async-start | bytes 4456448 | tf_op jit(solution)/shard_map/all_gather | solution.py:41
Sparse Core Ops, SparseCore 0:
  9.8 87.5 all-gather.3
  99.2 156.7 all-gather.5
  270.5 103.4 reduce-scatter.1
  399.6 77.4 all-gather.7
where the time goes:
time: 488 us
  waiting for transfers between devices  430 us (88%)
  blocking collectives  24.2 us (5%)
  matrix products  14.4 us (3%)
  between operations  13.8 us (3%)
    all_gather x2, waiting for transfers between devices, gathered_by_axis(): nearer = lax.all_gather(shard, axes[-1], axis=dim, tiled=True)  248 us
    reduce_scatter x1, waiting for transfers between devices, on_device(): lax.psum_scatter(delta.astype(jnp.float32).astype(jnp.bfloat16), 'rep', s...  104 us
    all_gather x1, waiting for transfers between devices, on_device(): weights = lax.all_gather(part, 'rep', axis=0, tiled=True)  77.6 us
    dot_general x1, matrix products, on_device(): jnp.einsum('td,tf->df', gathered_by_axis(activations, TP, 1)[0], cot_rows...  14.4 us
    all_to_all x1, blocking collectives, on_device(): lax.all_to_all(summed.astype(jnp.bfloat16), TP, split_axis=0, concat_axis...  12.9 us
    all_to_all x1, blocking collectives, on_device(): part = lax.all_to_all(rounded, TP, split_axis=1, concat_axis=0, tiled=True)  11.3 us
  transfers between devices with their start and end apart: 4, of which 4 were waited for; matrix products, arithmetic and copies ran while one was open for 0% of the time, Pallas kernels for 0%

commit v1 on v0

--- a/solution.py
+++ b/solution.py
@@ -38,7 +38,10 @@
     new_outer = outer_weights - outer_rate * (average + nesterov * new_momentum)
     rounded = new_outer.astype(jnp.bfloat16)
     part = lax.all_to_all(rounded, TP, split_axis=1, concat_axis=0, tiled=True)
-    weights = lax.all_gather(part, "rep", axis=0, tiled=True)
+    count = lax.axis_size("rep")
+    tiles = jnp.stack([part for _ in range(count)])
+    tiles = lax.all_to_all(tiles, "rep", split_axis=0, concat_axis=0)
+    weights = jnp.concatenate(tiles, axis=0)
     return (weights, new_outer, new_momentum)
 
 

time: 488 us -> 516 us (1.057)
  blocking collectives: 24.2 us -> 128 us
  waiting for transfers between devices: 430 us -> 352 us
    all_to_all x0 -> x1, blocking collectives: none -> 104 us  [on_device(): tiles = lax.all_to_all(tiles, 'rep', split_axis=0, concat_axis=0)]
    all_gather x1 -> x0, waiting for transfers between devices: 77.6 us -> none  [on_device(): weights = lax.all_gather(part, 'rep', axis=0, tiled=True)]
  transfers between devices with their start and end apart: 4 -> 3, of which waited for: 4 -> 3; matrix products, arithmetic and copies ran while one was open for 0% -> 0% of each run, Pallas kernels for 0% -> 0%
where the time goes in v1:
time: 516 us; the launch traced here: 513 us
  waiting for transfers between devices  352 us (68%)
  blocking collectives  128 us (25%)
  matrix products  14.4 us (3%)
  between operations  13.8 us (3%)
    all_gather x2, waiting for transfers between devices, gathered_by_axis(): nearer = lax.all_gather(shard, axes[-1], axis=dim, tiled=True)  248 us
    all_to_all x1, blocking collectives, on_device(): tiles = lax.all_to_all(tiles, 'rep', split_axis=0, concat_axis=0)  104 us
    reduce_scatter x1, waiting for transfers between devices, on_device(): lax.psum_scatter(delta.astype(jnp.float32).astype(jnp.bfloat16), 'rep', s...  104 us
    dot_general x1, matrix products, on_device(): jnp.einsum('td,tf->df', gathered_by_axis(activations, TP, 1)[0], cot_rows...  14.4 us
    all_to_all x1, blocking collectives, on_device(): lax.all_to_all(summed.astype(jnp.bfloat16), TP, split_axis=0, concat_axis...  12.9 us
    all_to_all x1, blocking collectives, on_device(): part = lax.all_to_all(rounded, TP, split_axis=1, concat_axis=0, tiled=True)  11.3 us
  transfers between devices with their start and end apart: 3, of which 3 were waited for; matrix products, arithmetic and copies ran while one was open for 0% of the time, Pallas kernels for 0%

profile of v1, /device:TPU:1, one launch (start us, length us, event | category | flops | bytes accessed | tf_op | source)
XLA Modules:
  0.0 512.7 jit_solution(13424773250323593053)
XLA Ops:
  7.2 0.0 copy-start
  7.2 0.0 all-gather.3.cloned.1.call-start
  7.2 0.7 all-gather.3.cloned.1.call-update
  7.9 0.0 all-gather.5.cloned.1.call-start
  8.0 89.4 %all-gather.3.cloned.1.call-done = bf16[1,512,4096]{2,1,0:T(8,128)(2,1)} async-done(((bf16[1,128,4096]{2,1,0:T(8,128)(2,1)}), bf16[1,512,4096]{2,1,0:T(8,128)(2,1)}) %all-gather.3.cloned.1.call-update) | async-done | bytes 4194320 | tf_op jit(solution)/shard_map/all_gather | solution.py:16
  97.4 0.0 all-gather.5.cloned.1.call-update
  97.4 0.0 reduce-scatter.2.cloned.1.call-start
  97.4 158.5 %all-gather.5.cloned.1.call-done = bf16[1,2048,4096]{2,1,0:T(8,128)(2,1)} async-done(((bf16[1,512,4096]{2,1,0:T(8,128)(2,1)}), bf16[1,2048,4096]{2,1,0:T(8,128)(2,1)}) %all-gather.5.cloned.1.call-update) | async-done | bytes 16777232 | tf_op jit(solution)/shard_map/all_gather | solution.py:16
  255.9 0.0 copy-done
  255.9 14.4 %fusion.2 = bf16[4096,512]{1,0:T(8,128)(2,1)} fusion(bf16[1,2048,4096]{2,1,0:T(8,128)(2,1)} %all-gather.5.cloned.1.call-done, bf16[1,4096,512]{2,1,0:T(8,128)(2,1)} %param.7, bf16[1,2048,512]{2,1,0:T(8,128)(2,1)S(1)} %copy-done), kind=kOutput, calls=%fused_computation.3 | convolution fusion | flops 8596226048 | bytes 27262976 | tf_op jit(solution)/shard_map/td,tf->df/dot_general | solution.py:23
  270.4 0.0 copy-start.1
  270.4 0.0 copy-start.2
  270.4 0.0 reduce-scatter.2.cloned.1.call-update
  270.4 103.6 %reduce-scatter.2.cloned.1.call-done = bf16[256,512]{1,0:T(8,128)(2,1)} async-done(((bf16[4096,512]{1,0:T(8,128)(2,1)}), bf16[256,512]{1,0:T(8,128)(2,1)}) %reduce-scatter.2.cloned.1.call-update) | async-done | bytes 262160 | tf_op jit(solution)/shard_map/reduce_scatter | solution.py:30
  374.0 12.9 %all_to_all.34 = bf16[16,16,512]{2,1,0:T(8,128)(2,1)S(1)} all-to-all(bf16[16,16,512]{2,1,0:T(8,128)(2,1)} %bitcast.29), channel_id=1, replica_groups=mesh['rep'=16,'tp_0'=4,'tp_1'=4] {'tp_0','tp_1'}, dimensions={0} | all-to-all | bytes 524288 | tf_op jit(solution)/shard_map/all_to_all | solution.py:33
  386.9 0.1 multiply_bitcast_fusion
  387.0 0.0 copy-done.1
  387.0 0.0 copy-done.2
  387.0 1.1 fusion.6
  388.1 11.3 %all_to_all.35 = bf16[16,16,512]{2,0,1:T(8,128)(2,1)S(1)} all-to-all(bf16[16,16,512]{2,0,1:T(8,128)(2,1)S(1)} %bitcast.27), channel_id=1, replica_groups=mesh['rep'=16,'tp_0'=4,'tp_1'=4] {'tp_0','tp_1'}, dimensions={1} | all-to-all | bytes 524288 | tf_op jit(solution)/shard_map/all_to_all | solution.py:40
  399.4 0.4 stack.5
  399.8 104.3 %all_to_all.36 = bf16[16,256,512]{2,1,0:T(8,128)(2,1)S(1)} all-to-all(bf16[16,256,512]{2,1,0:T(8,128)(2,1)S(1)} %stack.5), channel_id=1, replica_groups=mesh['rep'=16,'tp_0'=4,'tp_1'=4] {'rep'}, dimensions={0} | all-to-all | bytes 8388608 | tf_op jit(solution)/shard_map/all_to_all | solution.py:43
  504.1 2.0 copy.19
  (2 shorter events, 0.1 us)
Async XLA Ops:
  7.2 248.8 %copy-start = (bf16[1,2048,512]{2,1,0:T(8,128)(2,1)S(1)}, bf16[1,2048,512]{2,1,0:T(8,128)(2,1)}, u32[]{:S(2)}) copy-start(bf16[1,2048,512]{2,1,0:T(8,128)(2,1)} %param.6) | copy-start | bytes 6291460
  7.2 90.2 %all-gather.3.cloned.1.call-start = ((), (), s32[]{:S(2)}) async-start(), calls=%async_computation.4 | async-start | bytes 5242880 | tf_op jit(solution)/shard_map/all_gather | solution.py:16
  7.9 248.0 %all-gather.5.cloned.1.call-start = ((), (), s32[]{:S(2)}) async-start(), calls=%async_computation.5 | async-start | bytes 20971520 | tf_op jit(solution)/shard_map/all_gather | solution.py:16
  97.4 276.6 %reduce-scatter.2.cloned.1.call-start = ((), (), s32[]{:S(2)}) async-start(), calls=%async_computation.6 | async-start | bytes 4456448 | tf_op jit(solution)/shard_map/reduce_scatter | solution.py:30
  270.4 116.6 %copy-start.1 = (f32[16,8192]{1,0:T(8,128)S(1)}, f32[16,8192]{1,0:T(8,128)}, u32[]{:S(2)}) copy-start(f32[16,8192]{1,0:T(8,128)} %param.8) | copy-start | bytes 1572868
  270.4 116.6 %copy-start.2 = (f32[16,8192]{1,0:T(8,128)S(1)}, f32[16,8192]{1,0:T(8,128)}, u32[]{:S(2)}) copy-start(f32[16,8192]{1,0:T(8,128)} %param.9) | copy-start | bytes 1572868
Sparse Core Ops, SparseCore 0:
  9.8 87.5 all-gather.2
  99.2 156.7 all-gather.4
  270.5 103.4 reduce-scatter.1
